TPU v7x, 32 devices: a whole 2x2x4 slice. The times are simulated.
32 devices in a mesh: blk: 8 (over z, x), tgt: 4 (over y, core).
Axes of the slice: x: 2, y: 2, z: 4, core: 2. Of those that a mesh axis runs over, the one named last changes fastest.
Arguments:
- sources: float32 [8192, 128], P('blk'), may hold values from -0.5 to 0.5, as said below
- targets: float32 [8192, 128], P(('blk', 'tgt')), may hold values from -0.5 to 0.5, as said below
- duals_init: float32 [8192], P(('blk', 'tgt')), may hold values from -1.5 to 1.5
Outputs:
- source_duals: float32 [8192], P('blk')
- target_duals: float32 [8192], P(('blk', 'tgt'))
Inputs may be any that keep to these rules, and one draw needn't show every extreme that they name: `sources`: coordinates of the source points. `targets`: coordinates of the target points.
All inputs are finite; a program needn't handle non-finite values.
Results may differ from a plain program's by a relative error of at most 0.0001.
Values sent between devices are 32-bit elements; how exact they have to be, the bound alone decides.
A program may use at most 64 MiB of HBM per device.

v0:
```python
import jax
import jax.numpy as jnp
from jax import lax
from jax.sharding import PartitionSpec as P

ITERS = 2
EPS = 0.05


def cost_of(left, left_norm, right, right_norm):
    cross = jnp.dot(
        left, right.T, preferred_element_type=jnp.float32, precision=lax.Precision.HIGHEST
    )
    return left_norm[:, None] + right_norm[None, :] - 2.0 * cross


def body(sources, targets, duals_init):
    src_norm = jnp.sum(sources * sources, axis=1)
    rows_here = sources.shape[0]
    cols_here = targets.shape[0]
    total_dst = cols_here * lax.axis_size("blk") * lax.axis_size("tgt")
    total_src = rows_here * lax.axis_size("blk")
    target_pots = duals_init
    source_pots = jnp.zeros_like(src_norm)
    group_rows = lax.all_gather(targets, "blk", axis=0, tiled=True)
    group_norm = jnp.sum(group_rows * group_rows, axis=1)
    cost_tile = cost_of(sources, src_norm, group_rows, group_norm)
    for repeat in range(ITERS):
        group_pots = lax.all_gather(target_pots, "blk", axis=0, tiled=True)
        scores = (group_pots[None, :] - cost_tile) / EPS
        maxima = jnp.max(scores, axis=1)
        totals = jnp.sum(jnp.exp(scores - maxima[:, None]), axis=1)
        highest = lax.pmax(maxima, "tgt")
        totals = lax.psum(totals * jnp.exp(maxima - highest), "tgt")
        maxima = highest
        source_pots = EPS * -jnp.log(jnp.float32(total_dst)) - EPS * (maxima + jnp.log(totals))
        col_scores = (source_pots[:, None] - cost_tile) / EPS
        col_high = lax.pmax(jnp.max(col_scores, axis=0), "blk")
        col_part = jnp.sum(jnp.exp(col_scores - col_high[None, :]), axis=0)
        col_total = lax.psum_scatter(col_part, "blk", scatter_dimension=0, tiled=True)
        own_high = lax.dynamic_slice_in_dim(
            col_high, lax.axis_index("blk") * cols_here, cols_here, 0
        )
        target_pots = EPS * -jnp.log(jnp.float32(total_src)) - EPS * (own_high + jnp.log(col_total))
    return (source_pots, target_pots)


def solution(mesh):
    return jax.shard_map(
        body,
        mesh=mesh,
        in_specs=(P("blk", None), P(("blk", "tgt"), None), P(("blk", "tgt"))),
        out_specs=(P("blk"), P(("blk", "tgt"))),
        check_vma=False,
    )
```

profile of v0, /device:TPU:0, one launch (start us, length us, event | category | flops | bytes accessed | tf_op | source)
XLA Modules:
  0.0 220.8 jit_solution(6186228106651673261)
XLA Ops:
  7.2 0.0 all-gather.4.cloned.1.call-start
  7.2 0.7 all-gather.4.cloned.1.call-update
  7.9 1.2 dynamic-slice
  9.8 22.5 %all-gather = f32[8,1,256]{2,1,0:T(1,128)S(1)} all-gather(f32[1,1,256]{2,1,0:T(1,128)} %bitcast.12), channel_id=1, replica_groups=mesh['blk'=8,'tgt'=4] {'blk'}, dimensions={0}, use_global_device_ids=true | all-gather | bytes 9216 | tf_op jit(solution)/shard_map/all_gather | solution.py:29
  32.3 1.2 multiply_reduce_fusion.1
  33.6 19.5 %all-gather.4.cloned.1.call-done = f32[2048,128]{1,0:T(8,128)} async-done(((f32[256,128]{1,0:T(8,128)}), f32[2048,128]{1,0:T(8,128)}) %all-gather.4.cloned.1.call-update) | async-done | bytes 1048592 | tf_op jit(solution)/shard_map/all_gather | solution.py:25
  53.1 1.6 multiply_reduce_fusion
  54.7 11.5 %fusion = (f32[1024]{0:T(1024)S(1)}, f32[1024,2048]{1,0:T(8,128)}) fusion(f32[2048]{0:T(1024)S(1)} %bitcast.9, f32[1024,128]{1,0:T(8,128)} %param.3, f32[2048,128]{1,0:T(8,128)} %all-gather.4.cloned.1.call-done, f32[2048]{0:T(1024)S(1)} %multiply_reduce_fusion, f32[1024]{0:T(1024)S(1)} %multiply_reduce_fusion.1), kind=kOutput, calls=%fused_computation.9 | convolution fusion | flops 3233807360 | bytes 9986048 | tf_op jit(solution)/shard_map/dot_general | solution.py:11
  66.2 5.6 %pmax.28 = f32[1024]{0:T(1024)S(1)} all-reduce(f32[1024]{0:T(1024)S(1)} %get-tuple-element.2), channel_id=1, replica_groups=mesh['blk'=8,'tgt'=4] {'tgt'}, use_global_device_ids=true, to_apply=%region_3.0 | all-reduce | flops 1024 | bytes 8192 | tf_op jit(solution)/shard_map/pmax | solution.py:33
  71.8 4.5 %exponential_reduce_fusion.3 = f32[1024]{0:T(1024)S(1)} fusion(f32[1024,2048]{1,0:T(8,128)} %get-tuple-element.3, f32[1024]{0:T(1024)S(1)} %get-tuple-element.2, f32[2048]{0:T(1024)S(1)} %bitcast.10), kind=kLoop, calls=%fused_computation.6 | loop fusion | flops 8387584 | bytes 8404992 | tf_op jit(solution)/shard_map/reduce_sum | solution.py:32
  76.4 6.6 %psum.14 = f32[1024]{0:T(1024)S(1)} all-reduce(f32[1024]{0:T(1024)S(1)} %exponential_multiply_fusion.1), channel_id=1, replica_groups=mesh['blk'=8,'tgt'=4] {'tgt'}, use_global_device_ids=true, to_apply=%region_5.0 | all-reduce | flops 1024 | bytes 8192 | tf_op jit(solution)/shard_map/psum | solution.py:34
  83.0 4.3 %fusion.1 = f32[2048]{0:T(1024)S(1)} fusion(f32[1024,2048]{1,0:T(8,128)} %get-tuple-element.3, f32[1024]{0:T(1024)S(1)} %multiply_subtract_fusion.2), kind=kLoop, calls=%fused_computation.10 | loop fusion | flops 6289408 | bytes 8400896 | tf_op jit(solution)/shard_map/reduce_max | solution.py:38
  87.3 19.4 %pmax.29 = f32[2048]{0:T(1024)S(1)} all-reduce(f32[2048]{0:T(1024)S(1)} %fusion.1), channel_id=1, replica_groups=mesh['blk'=8,'tgt'=4] {'blk'}, use_global_device_ids=true, to_apply=%region_7.0 | all-reduce | flops 2048 | bytes 16384 | tf_op jit(solution)/shard_map/pmax | solution.py:38
  106.7 4.5 %exponential_reduce_fusion.2 = f32[2048]{0:T(1024)S(1)} fusion(f32[1024,2048]{1,0:T(8,128)} %get-tuple-element.3, f32[2048]{0:T(1024)S(1)} %pmax.29, f32[1024]{0:T(1024)S(1)} %multiply_subtract_fusion.2), kind=kLoop, calls=%fused_computation.4 | loop fusion | flops 8386560 | bytes 8409088 | tf_op jit(solution)/shard_map/reduce_sum | solution.py:39
  111.2 17.4 %all-reduce = f32[2048]{0:T(1024)S(1)} all-reduce(f32[2048]{0:T(1024)S(1)} %exponential_reduce_fusion.2), channel_id=2, replica_groups=mesh['blk'=8,'tgt'=4] {'blk'}, use_global_device_ids=true, to_apply=%region_9.0.clone | all-reduce | flops 2048 | bytes 16384
  128.6 0.1 fusion.9
  128.7 18.2 %all-gather.1 = f32[8,1,256]{2,1,0:T(1,128)S(1)} all-gather(f32[1,1,256]{2,1,0:T(1,128)S(1)} %bitcast.11), channel_id=1, replica_groups=mesh['blk'=8,'tgt'=4] {'blk'}, dimensions={0}, use_global_device_ids=true | all-gather | bytes 9216 | tf_op jit(solution)/shard_map/all_gather | solution.py:29
  147.0 4.3 %fusion.2 = f32[1024]{0:T(1024)S(1)} fusion(f32[1024,2048]{1,0:T(8,128)} %get-tuple-element.3, f32[2048]{0:T(1024)S(1)} %bitcast.7), kind=kLoop, calls=%fused_computation.11 | loop fusion | flops 6290432 | bytes 8400896 | tf_op jit(solution)/shard_map/reduce_max | solution.py:31
  151.3 4.5 %exponential_reduce_fusion.1 = f32[1024]{0:T(1024)S(1)} fusion(f32[1024,2048]{1,0:T(8,128)} %get-tuple-element.3, f32[1024]{0:T(1024)S(1)} %fusion.2, f32[2048]{0:T(1024)S(1)} %bitcast.8), kind=kLoop, calls=%fused_computation.2 | loop fusion | flops 8387584 | bytes 8404992 | tf_op jit(solution)/shard_map/reduce_sum | solution.py:32
  155.8 5.7 %pmax.30 = f32[1024]{0:T(1024)S(1)} all-reduce(f32[1024]{0:T(1024)S(1)} %fusion.2), channel_id=1, replica_groups=mesh['blk'=8,'tgt'=4] {'tgt'}, use_global_device_ids=true, to_apply=%region_11.0 | all-reduce | flops 1024 | bytes 8192 | tf_op jit(solution)/shard_map/pmax | solution.py:33
  161.5 6.3 %psum.15 = f32[1024]{0:T(1024)S(1)} all-reduce(f32[1024]{0:T(1024)S(1)} %exponential_multiply_fusion), channel_id=1, replica_groups=mesh['blk'=8,'tgt'=4] {'tgt'}, use_global_device_ids=true, to_apply=%region_13.0 | all-reduce | flops 1024 | bytes 8192 | tf_op jit(solution)/shard_map/psum | solution.py:34
  167.7 0.0 copy-start
  167.7 4.3 %fusion.3 = f32[2048]{0:T(1024)S(1)} fusion(f32[1024,2048]{1,0:T(8,128)} %get-tuple-element.3, f32[1024]{0:T(1024)S(1)} %multiply_subtract_fusion.1), kind=kLoop, calls=%fused_computation.12 | loop fusion | flops 6289408 | bytes 8400896 | tf_op jit(solution)/shard_map/reduce_max | solution.py:38
  172.0 17.4 %pmax.31 = f32[2048]{0:T(1024)S(1)} all-reduce(f32[2048]{0:T(1024)S(1)} %fusion.3), channel_id=1, replica_groups=mesh['blk'=8,'tgt'=4] {'blk'}, use_global_device_ids=true, to_apply=%region_15.0 | all-reduce | flops 2048 | bytes 16384 | tf_op jit(solution)/shard_map/pmax | solution.py:38
  189.4 4.5 %exponential_reduce_fusion = f32[2048]{0:T(1024)S(1)} fusion(f32[1024,2048]{1,0:T(8,128)} %get-tuple-element.3, f32[2048]{0:T(1024)S(1)} %pmax.31, f32[1024]{0:T(1024)S(1)} %multiply_subtract_fusion.1), kind=kLoop, calls=%fused_computation | loop fusion | flops 8386560 | bytes 8409088 | tf_op jit(solution)/shard_map/reduce_sum | solution.py:39
  193.9 0.0 copy-done
  193.9 19.4 %all-reduce.1 = f32[2048]{0:T(1024)S(1)} all-reduce(f32[2048]{0:T(1024)S(1)} %exponential_reduce_fusion), channel_id=3, replica_groups=mesh['blk'=8,'tgt'=4] {'blk'}, use_global_device_ids=true, to_apply=%region_17.0.clone | all-reduce | flops 2048 | bytes 16384
  213.3 0.7 fusion.6
  (4 shorter events, 0.0 us)
Async XLA Ops:
  7.2 46.0 %all-gather.4.cloned.1.call-start = ((), (), s32[]{:S(2)}) async-start(), calls=%async_computation | async-start | bytes 1179648 | tf_op jit(solution)/shard_map/all_gather | solution.py:25
  167.7 26.2 %copy-start = (f32[1024]{0:T(1024)}, f32[1024]{0:T(1024)S(1)}, u32[]{:S(2)}) copy-start(f32[1024]{0:T(1024)S(1)} %multiply_subtract_fusion.1) | copy-start | bytes 12292
Sparse Core Ops, SparseCore 0:
  10.1 42.9 all-gather.3
where the time goes:
time: 221 us
  blocking collectives  139 us (63%)
  other arithmetic  34.5 us (16%)
  waiting for transfers between devices  20.2 us (9%)
  between operations  14.8 us (7%)
  matrix products  11.5 us (5%)
    all_gather x2, blocking collectives, body(): group_pots = lax.all_gather(target_pots, 'blk', axis=0, tiled=True)  40.8 us
    unnamed x2, blocking collectives  36.8 us
    pmax x2, blocking collectives, body(): col_high = lax.pmax(jnp.max(col_scores, axis=0), 'blk')  36.8 us
    all_gather x1, waiting for transfers between devices, body(): group_rows = lax.all_gather(targets, 'blk', axis=0, tiled=True)  19.5 us
    psum x2, blocking collectives, body(): totals = lax.psum(totals * jnp.exp(maxima - highest), 'tgt')  12.9 us
    dot_general x1, matrix products, cost_of(): jnp.dot(left, right.T, preferred_element_type=jnp.float32, precision=lax....  11.5 us
    pmax x2, blocking collectives, body(): highest = lax.pmax(maxima, 'tgt')  11.3 us
    reduce_sum x2, other arithmetic, body(): totals = jnp.sum(jnp.exp(scores - maxima[:, None]), axis=1)  9.01 us
  transfers between devices with their start and end apart: 1, of which 1 were waited for; matrix products, arithmetic and copies ran while one was open for 1% of the time, Pallas kernels for 0%

commit v1 on v0

--- a/solution.py
+++ b/solution.py
@@ -31,7 +31,9 @@
         maxima = jnp.max(scores, axis=1)
         totals = jnp.sum(jnp.exp(scores - maxima[:, None]), axis=1)
         highest = lax.pmax(maxima, "tgt")
-        totals = lax.psum(totals * jnp.exp(maxima - highest), "tgt")
+        block = totals * jnp.exp(maxima - highest)
+        parts = lax.all_gather(block, "tgt")
+        totals = jnp.sum(parts, axis=0)
         maxima = highest
         source_pots = EPS * -jnp.log(jnp.float32(total_dst)) - EPS * (maxima + jnp.log(totals))
         col_scores = (source_pots[:, None] - cost_tile) / EPS

time: 221 us -> 219 us (level)
  blocking collectives: 139 us -> 136 us
    psum x2 -> x0, blocking collectives: 12.9 us -> none  [body(): totals = lax.psum(totals * jnp.exp(maxima - highest), 'tgt')]
    all_gather x0 -> x2, blocking collectives: none -> 10.6 us  [body(): parts = lax.all_gather(block, 'tgt')]
where the time goes in v1:
time: 219 us
  blocking collectives  136 us (62%)
  other arithmetic  34.5 us (16%)
  waiting for transfers between devices  20.2 us (9%)
  between operations  14.8 us (7%)
  matrix products  11.5 us (5%)
    all_gather x2, blocking collectives, body(): group_pots = lax.all_gather(target_pots, 'blk', axis=0, tiled=True)  40.8 us
    pmax x2, blocking collectives, body(): col_high = lax.pmax(jnp.max(col_scores, axis=0), 'blk')  36.8 us
    unnamed x2, blocking collectives  36.8 us
    all_gather x1, waiting for transfers between devices, body(): group_rows = lax.all_gather(targets, 'blk', axis=0, tiled=True)  19.5 us
    dot_general x1, matrix products, cost_of(): jnp.dot(left, right.T, preferred_element_type=jnp.float32, precision=lax....  11.5 us
    pmax x2, blocking collectives, body(): highest = lax.pmax(maxima, 'tgt')  11.3 us
    all_gather x2, blocking collectives, body(): parts = lax.all_gather(block, 'tgt')  10.6 us
    reduce_sum x2, other arithmetic, body(): col_part = jnp.sum(jnp.exp(col_scores - col_high[None, :]), axis=0)  9.01 us
  transfers between devices with their start and end apart: 1, of which 1 were waited for; matrix products, arithmetic and copies ran while one was open for 1% of the time, Pallas kernels for 0%

profile of v1, /device:TPU:0, one launch (start us, length us, event | category | flops | bytes accessed | tf_op | source)
XLA Modules:
  0.0 218.6 jit_solution(49708795191288008)
XLA Ops:
  7.2 0.0 all-gather.6.cloned.1.call-start
  7.2 0.7 all-gather.6.cloned.1.call-update
  7.9 1.2 dynamic-slice
  9.8 22.5 %all-gather.2 = f32[8,1,256]{2,1,0:T(1,128)S(1)} all-gather(f32[1,1,256]{2,1,0:T(1,128)} %bitcast.12), channel_id=1, replica_groups=mesh['blk'=8,'tgt'=4] {'blk'}, dimensions={0}, use_global_device_ids=true | all-gather | bytes 9216 | tf_op jit(solution)/shard_map/all_gather | solution.py:29
  32.3 1.2 multiply_reduce_fusion.1
  33.6 19.5 %all-gather.6.cloned.1.call-done = f32[2048,128]{1,0:T(8,128)} async-done(((f32[256,128]{1,0:T(8,128)}), f32[2048,128]{1,0:T(8,128)}) %all-gather.6.cloned.1.call-update) | async-done | bytes 1048592 | tf_op jit(solution)/shard_map/all_gather | solution.py:25
  53.1 1.6 multiply_reduce_fusion
  54.7 11.5 %fusion = (f32[1024]{0:T(1024)S(1)}, f32[1024,2048]{1,0:T(8,128)}) fusion(f32[2048]{0:T(1024)S(1)} %bitcast.9, f32[1024,128]{1,0:T(8,128)} %param.3, f32[2048,128]{1,0:T(8,128)} %all-gather.6.cloned.1.call-done, f32[2048]{0:T(1024)S(1)} %multiply_reduce_fusion, f32[1024]{0:T(1024)S(1)} %multiply_reduce_fusion.1), kind=kOutput, calls=%fused_computation.9 | convolution fusion | flops 3233807360 | bytes 9986048 | tf_op jit(solution)/shard_map/dot_general | solution.py:11
  66.2 5.6 %pmax.28 = f32[1024]{0:T(1024)S(1)} all-reduce(f32[1024]{0:T(1024)S(1)} %get-tuple-element.2), channel_id=1, replica_groups=mesh['blk'=8,'tgt'=4] {'tgt'}, use_global_device_ids=true, to_apply=%region_3.0 | all-reduce | flops 1024 | bytes 8192 | tf_op jit(solution)/shard_map/pmax | solution.py:33
  71.8 4.5 %exponential_reduce_fusion.3 = f32[1024]{0:T(1024)S(1)} fusion(f32[1024,2048]{1,0:T(8,128)} %get-tuple-element.3, f32[1024]{0:T(1024)S(1)} %get-tuple-element.2, f32[2048]{0:T(1024)S(1)} %bitcast.10), kind=kLoop, calls=%fused_computation.6 | loop fusion | flops 8387584 | bytes 8404992 | tf_op jit(solution)/shard_map/reduce_sum | solution.py:32
  76.4 5.2 %all-gather = f32[4096]{0:T(1024)S(1)} all-gather(f32[1024]{0:T(1024)S(1)} %exponential_multiply_fusion.1), channel_id=2, replica_groups=mesh['blk'=8,'tgt'=4] {'tgt'}, dimensions={0}, use_global_device_ids=true | all-gather | bytes 20480 | tf_op jit(solution)/shard_map/all_gather | solution.py:35
  81.6 4.3 %fusion.1 = f32[2048]{0:T(1024)S(1)} fusion(f32[1024,2048]{1,0:T(8,128)} %get-tuple-element.3, f32[1024]{0:T(1024)S(1)} %multiply_subtract_fusion.2), kind=kLoop, calls=%fused_computation.10 | loop fusion | flops 6289408 | bytes 8400896 | tf_op jit(solution)/shard_map/reduce_max | solution.py:40
  85.9 19.4 %pmax.29 = f32[2048]{0:T(1024)S(1)} all-reduce(f32[2048]{0:T(1024)S(1)} %fusion.1), channel_id=1, replica_groups=mesh['blk'=8,'tgt'=4] {'blk'}, use_global_device_ids=true, to_apply=%region_7.0 | all-reduce | flops 2048 | bytes 16384 | tf_op jit(solution)/shard_map/pmax | solution.py:40
  105.3 4.5 %exponential_reduce_fusion.2 = f32[2048]{0:T(1024)S(1)} fusion(f32[1024,2048]{1,0:T(8,128)} %get-tuple-element.3, f32[2048]{0:T(1024)S(1)} %pmax.29, f32[1024]{0:T(1024)S(1)} %multiply_subtract_fusion.2), kind=kLoop, calls=%fused_computation.4 | loop fusion | flops 8386560 | bytes 8409088 | tf_op jit(solution)/shard_map/reduce_sum | solution.py:41
  109.8 17.4 %all-reduce = f32[2048]{0:T(1024)S(1)} all-reduce(f32[2048]{0:T(1024)S(1)} %exponential_reduce_fusion.2), channel_id=4, replica_groups=mesh['blk'=8,'tgt'=4] {'blk'}, use_global_device_ids=true, to_apply=%region_9.0.clone | all-reduce | flops 2048 | bytes 16384
  127.2 0.1 fusion.9
  127.3 18.3 %all-gather.3 = f32[8,1,256]{2,1,0:T(1,128)S(1)} all-gather(f32[1,1,256]{2,1,0:T(1,128)S(1)} %bitcast.11), channel_id=1, replica_groups=mesh['blk'=8,'tgt'=4] {'blk'}, dimensions={0}, use_global_device_ids=true | all-gather | bytes 9216 | tf_op jit(solution)/shard_map/all_gather | solution.py:29
  145.6 4.3 %fusion.2 = f32[1024]{0:T(1024)S(1)} fusion(f32[1024,2048]{1,0:T(8,128)} %get-tuple-element.3, f32[2048]{0:T(1024)S(1)} %bitcast.7), kind=kLoop, calls=%fused_computation.11 | loop fusion | flops 6290432 | bytes 8400896 | tf_op jit(solution)/shard_map/reduce_max | solution.py:31
  149.9 4.5 %exponential_reduce_fusion.1 = f32[1024]{0:T(1024)S(1)} fusion(f32[1024,2048]{1,0:T(8,128)} %get-tuple-element.3, f32[1024]{0:T(1024)S(1)} %fusion.2, f32[2048]{0:T(1024)S(1)} %bitcast.8), kind=kLoop, calls=%fused_computation.2 | loop fusion | flops 8387584 | bytes 8404992 | tf_op jit(solution)/shard_map/reduce_sum | solution.py:32
  154.4 5.7 %pmax.30 = f32[1024]{0:T(1024)S(1)} all-reduce(f32[1024]{0:T(1024)S(1)} %fusion.2), channel_id=1, replica_groups=mesh['blk'=8,'tgt'=4] {'tgt'}, use_global_device_ids=true, to_apply=%region_11.0 | all-reduce | flops 1024 | bytes 8192 | tf_op jit(solution)/shard_map/pmax | solution.py:33
  160.1 5.4 %all-gather.1 = f32[4096]{0:T(1024)S(1)} all-gather(f32[1024]{0:T(1024)S(1)} %exponential_multiply_fusion), channel_id=3, replica_groups=mesh['blk'=8,'tgt'=4] {'tgt'}, dimensions={0}, use_global_device_ids=true | all-gather | bytes 20480 | tf_op jit(solution)/shard_map/all_gather | solution.py:35
  165.5 0.0 copy-start
  165.5 4.3 %fusion.3 = f32[2048]{0:T(1024)S(1)} fusion(f32[1024,2048]{1,0:T(8,128)} %get-tuple-element.3, f32[1024]{0:T(1024)S(1)} %multiply_subtract_fusion.1), kind=kLoop, calls=%fused_computation.12 | loop fusion | flops 6289408 | bytes 8400896 | tf_op jit(solution)/shard_map/reduce_max | solution.py:40
  169.8 17.4 %pmax.31 = f32[2048]{0:T(1024)S(1)} all-reduce(f32[2048]{0:T(1024)S(1)} %fusion.3), channel_id=1, replica_groups=mesh['blk'=8,'tgt'=4] {'blk'}, use_global_device_ids=true, to_apply=%region_15.0 | all-reduce | flops 2048 | bytes 16384 | tf_op jit(solution)/shard_map/pmax | solution.py:40
  187.2 4.5 %exponential_reduce_fusion = f32[2048]{0:T(1024)S(1)} fusion(f32[1024,2048]{1,0:T(8,128)} %get-tuple-element.3, f32[2048]{0:T(1024)S(1)} %pmax.31, f32[1024]{0:T(1024)S(1)} %multiply_subtract_fusion.1), kind=kLoop, calls=%fused_computation | loop fusion | flops 8386560 | bytes 8409088 | tf_op jit(solution)/shard_map/reduce_sum | solution.py:41
  191.7 0.0 copy-done
  191.7 19.4 %all-reduce.1 = f32[2048]{0:T(1024)S(1)} all-reduce(f32[2048]{0:T(1024)S(1)} %exponential_reduce_fusion), channel_id=5, replica_groups=mesh['blk'=8,'tgt'=4] {'blk'}, use_global_device_ids=true, to_apply=%region_17.0.clone | all-reduce | flops 2048 | bytes 16384
  211.1 0.7 fusion.6
  (8 shorter events, 0.1 us)
Async XLA Ops:
  7.2 46.0 %all-gather.6.cloned.1.call-start = ((), (), s32[]{:S(2)}) async-start(), calls=%async_computation | async-start | bytes 1179648 | tf_op jit(solution)/shard_map/all_gather | solution.py:25
  165.5 26.2 %copy-start = (f32[1024]{0:T(1024)}, f32[1024]{0:T(1024)S(1)}, u32[]{:S(2)}) copy-start(f32[1024]{0:T(1024)S(1)} %multiply_subtract_fusion.1) | copy-start | bytes 12292
Sparse Core Ops, SparseCore 0:
  10.1 42.9 all-gather.5
